TPU v7x, 8 devices: a whole 2x2x1 slice. The times are simulated.
8 devices in a mesh: dp: 2 (over z, y), ep: 4 (over x, core).
Axes of the slice: x: 2, y: 2, z: 1, core: 2. Of those that a mesh axis runs over, the one named last changes fastest.
Arguments:
- tok_x: bfloat16 [512, 2048], P(('dp', 'ep')), parts along dimension 0
- route_ids: int32 [512, 8], P(('dp', 'ep')), parts along dimension 0
- route_gate: float32 [512, 8], P(('dp', 'ep')), parts along dimension 0
- w_in: bfloat16 [128, 2048, 768], P('ep')
- w_out: bfloat16 [128, 768, 2048], P('ep')
- shared_in: bfloat16 [2048, 768], replicated
- shared_out: bfloat16 [768, 2048], replicated
Outputs:
- output: bfloat16 [512, 2048], P(('dp', 'ep')), parts along dimension 0
There are 2 independent parts. A program takes and returns all parts, laid end to end along the dimension named above; an argument that names none is the same for every part.
All inputs are finite; a program needn't handle non-finite values.
Results may differ from a plain program's by a relative error of at most 0.00521982.
Values are sent between devices in bfloat16 or wider.
A program may use at most 1 GiB of HBM per device.

v0:
```python
import jax
import jax.numpy as jnp
from jax import lax
from jax.experimental import pallas as pl
from jax.experimental.pallas import tpu as pltpu
from jax.sharding import PartitionSpec as P

F32 = jnp.float32
BF16 = jnp.bfloat16
MESH = pl.DeviceIdType.MESH

ROWS = 64
WIDTH = 2048
FF = 768
TOPK = 8
LOCAL = 16
CAP = 16
H = 128
T = 256
NCH = WIDTH // T
EG = 4
KS = 2 * T
NK = WIDTH // KS
NEG = LOCAL // EG
EB = 8
NHB = LOCAL // EB
NF = FF // T
GROUP = 256
NS = 13
A_STEPS = NK * NEG
B_STEPS = NCH * NHB
SH_IN = A_STEPS + B_STEPS
SH_OUT = SH_IN + 1
STEPS = SH_OUT + 1
LAG2 = 3


def dot(a, b):
    return jnp.dot(a, b, preferred_element_type=F32)


def tdot(a, b):
    return lax.dot_general(a, b, (((0,), (0,)), ((), ())), preferred_element_type=F32)


def bdot(a, b):
    return lax.dot_general(a, b, (((2,), (1,)), ((0,), (0,))), preferred_element_type=F32)


def kernel(x_ref, ids_ref, gates_ref, win_ref, wout_ref, wpair_ref, sin_ref, sout_ref, o_ref,
           tok, mids, mgates, ring, xs, hacc, hid, hid3, osc, disp, comb, comb3, ypart, r0, r1, r2, hs, shy,
           ld_sem, rts, rtr, g1s, g1r, g2s, g2r, gds, gdr, w_sem, t0s, t0r, t1s, t1r, t2s, fin):
    my_dp = lax.axis_index('dp')
    my_ep = lax.axis_index('ep')
    my_x = my_ep // 2
    my_c = my_ep % 2
    my_pos = my_c * 4 + my_dp * 2 + my_x
    partner = (my_dp, my_x * 2 + (1 - my_c))
    x_nbr = (my_dp, (1 - my_x) * 2 + my_c)
    y_nbr = (1 - my_dp, my_ep)
    e_off = my_dp * LOCAL

    def wait_all(ref, sem):
        pltpu.make_async_copy(ref, ref, sem).wait()

    def w_copies(s):
        slot = s % NS
        if s == SH_OUT:
            return [pltpu.make_async_copy(
                sout_ref.at[:, :, pl.ds(c * T, T)], ring.at[slot, :, c // 2, c % 2], w_sem.at[slot]) for c in range(NCH)]
        copies = []
        for n in range(NF):
            if s < A_STEPS:
                k, eg = divmod(s, NEG)
                src = win_ref.at[pl.ds(e_off + eg * EG, EG), pl.ds(2 * k, 2), :, pl.ds(n * T, T)]
            elif s < SH_IN:
                c, h = divmod(s - A_STEPS, NHB)
                if n < 2:
                    src = wout_ref.at[pl.ds(e_off + h * EB + n * EG, EG), pl.ds(0, 2), :, pl.ds(c * T, T)]
                else:
                    src = wpair_ref.at[pl.ds(e_off // 2 + h * EG, EG), :, 2, :, pl.ds(c * T, T)]
            else:
                src = sin_ref.at[:, :, :, pl.ds(n * T, T)]
            copies.append(pltpu.make_async_copy(src, ring.at[slot, n], w_sem.at[slot]))
        return copies

    def w_start(s):
        if s < STEPS:
            for copy in w_copies(s):
                copy.start()

    def w_wait(s):
        wait_all(ring.at[s % NS], w_sem.at[s % NS])

    IDS, GATES = NCH, NCH + 1

    def over_y(i):
        return i % 2 == 1

    def own_core(i):
        return tok.at[i, my_c]

    def own_pair(i):
        return tok.at[i, my_c, my_x if over_y(i) else my_dp]

    def own(i):
        if i == IDS:
            return mids.at[my_pos]
        if i == GATES:
            return mgates.at[my_pos]
        return tok.at[i, my_c, my_x, my_dp] if over_y(i) else tok.at[i, my_c, my_dp, my_x]

    def load(i):
        src = ids_ref if i == IDS else gates_ref if i == GATES else x_ref.at[:, pl.ds(i * T, T)]
        return pltpu.make_async_copy(src, own(i), ld_sem.at[max(0, i - NCH + 1)])

    def remote(src, dst, ssem, rsem, dev):
        return pltpu.make_async_remote_copy(
            src_ref=src, dst_ref=dst, send_sem=ssem, recv_sem=rsem, device_id=dev, device_id_type=MESH)

    def gather1(i):
        return remote(own(i), own(i), g1s, g1r.at[i // 2], y_nbr if over_y(i) else x_nbr)

    def gather2(i):
        return remote(own_pair(i), own_pair(i), g2s, g2r.at[i // 2], x_nbr if over_y(i) else y_nbr)

    def gatherd(i):
        return remote(own_core(i), own_core(i), gds, gdr.at[i // 2], partner)

    routing = [IDS, GATES]
    items = routing + list(range(NCH))

    def peer(r):
        dp = 1 - my_dp if r & 1 else my_dp
        x = 1 - my_x if r & 2 else my_x
        c = 1 - my_c if r & 4 else my_c
        return dp, x * 2 + c

    def tell(i, r):
        return remote(own(i), own(i), rts.at[i - NCH], rtr.at[i - NCH], peer(r))

    barrier = pltpu.get_barrier_semaphore()
    for r in range(1, 8):
        pl.semaphore_signal(barrier, inc=1, device_id=peer(r), device_id_type=MESH)
    for i in items:
        load(i).start()
    hid3[...] = jnp.zeros_like(hid3)
    wait_all(tok.at[0], ld_sem.at[0])
    for i in routing:
        load(i).wait()
    for s in range(NS):
        w_start(s)
    pl.semaphore_wait(barrier, 7)

    def direct(i, r):
        return remote(own(i), own(i), g1s, g2r.at[0], peer(r))

    def send(p):
        for i in (2 * p, 2 * p + 1):
            gather1(i).start()

    def send_on(p):
        wait_all(tok.at[2 * p, 0, 0], g1r.at[p])
        for i in (2 * p, 2 * p + 1):
            gather2(i).start()

    def share(p):
        wait_all(tok.at[pl.ds(0, 3), 0, 0] if p == 0 else tok.at[2 * p, 0], g2r.at[p])
        for i in (2 * p, 2 * p + 1):
            gatherd(i).start()

    for r in (3, 7, 1, 2, 5, 6, 4):
        for i in routing:
            tell(i, r).start()
    for r in (3, 2, 1):
        for i in (0, 1):
            direct(i, r).start()
    send(1)
    wait_all(mids.at[pl.ds(0, 7)], rtr.at[0])
    wait_all(mgates.at[pl.ds(0, 7)], rtr.at[1])

    e_id = lax.broadcasted_iota(jnp.int32, (LOCAL, GROUP), 0) + (my_ep * (2 * LOCAL) + e_off)
    s_id = lax.broadcasted_iota(jnp.int32, (LOCAL, CAP, GROUP), 1).astype(F32)

    def true_pos(t):
        return ((t // 64) % 2) * 128 + (t // 128) * 64 + t % 64

    t_row = lax.broadcasted_iota(jnp.int32, (GROUP, GROUP), 0)
    t_col = lax.broadcasted_iota(jnp.int32, (GROUP, GROUP), 1)
    before = jnp.where(true_pos(t_row) < true_pos(t_col), 1.0, 0.0).astype(BF16)
    eye = jnp.where(t_row == t_col, 1.0, 0.0).astype(BF16)
    for g in range(2):
        ids = jnp.concatenate([mids[c * 4 + g * 2 + x] for c in range(2) for x in range(2)], axis=1)
        gates = jnp.concatenate([mgates[c * 4 + g * 2 + x] for c in range(2) for x in range(2)], axis=1)
        chosen = jnp.zeros((LOCAL, GROUP), F32)
        gate = jnp.zeros((LOCAL, GROUP), F32)
        for j in range(TOPK):
            hit = ids[j:j + 1, :] == e_id
            chosen = jnp.where(hit, 1.0, chosen)
            gate = jnp.where(hit, gates[j:j + 1, :], gate)
        slot = dot(chosen.astype(BF16), before)
        slot = jnp.where(chosen > 0.0, slot, -1.0)
        here = slot[:, None, :] == s_id
        disp[g] = jnp.where(here, 1.0, 0.0).reshape(LOCAL * CAP, GROUP).astype(BF16)
        weight = jnp.where(here, gate[:, None, :], 0.0).reshape(LOCAL * CAP, GROUP)
        for piece in range(3):
            part = weight.astype(BF16)
            turned = tdot(part, eye).astype(BF16)
            if piece < 2:
                comb[g, :, pl.ds(piece * GROUP, GROUP)] = turned
            else:
                comb3[g] = turned
            weight = weight - part.astype(F32)

    send(2)
    send(3)
    send_on(1)
    share(0)
    for k in range(NK):
        wait_all(tok.at[2 * k], gdr.at[k])
        for h in range(2):
            i = 2 * k + h
            for g in range(2):
                rows = tok[i, :, :, g] if over_y(i) else tok[i, :, g]
                picked = dot(disp[g], rows.reshape(GROUP, T)).astype(BF16)
                xs[:, pl.ds(g * CAP, CAP), pl.ds(h * T, T)] = picked.reshape(LOCAL, CAP, T)
        for half in range(2):
            steps = [k * NEG + half * 2 + q for q in range(2)]
            for s in steps:
                w_wait(s)
            for s in steps:
                eg = s % NEG
                batch = pl.ds(eg * EG, EG)
                for n in range(NF):
                    cols = pl.ds(n * T, T)
                    acc = bdot(xs[batch], ring[s % NS, n].reshape(EG, KS, T))
                    if k > 0:
                        acc = acc + hacc[batch, :, cols]
                    if k < NK - 1:
                        hacc[batch, :, cols] = acc
                        continue
                    act = jax.nn.gelu(acc).astype(BF16)
                    if n < 2:
                        hid[batch, :, cols] = act
                    else:
                        act = act.reshape(EG // 2, 2, 2 * CAP, T)
                        for m in range(2):
                            hid3[pl.ds(eg * EG // 2, EG // 2), pl.ds(m * 2 * CAP, 2 * CAP), pl.ds(m * T, T)] = act[:, m]
            for s in steps:
                w_start(s + NS)
            if half == 0 and k < NK - 1:
                if k == 0:
                    send_on(2)
                    send_on(3)
                share(k + 1)

    def route(d):
        if d == 0:
            return my_x, my_dp, x_nbr, y_nbr
        return my_dp, my_x, y_nbr, x_nbr

    def reduce0(c):
        return remote(ypart.at[c, 1 - my_c], r0.at[c], t0s, t0r.at[c], partner)

    def reduce1(c, d, last):
        a, b, dev, _ = route(d)
        side = b if last else 1 - b
        return remote(ypart.at[c, my_c, d, 1 - a, side], r1.at[c, d, side], t1s, fin.at[c] if last else t1r.at[c], dev)

    def reduce2(c, d):
        a, b, _, dev = route(d)
        return remote(ypart.at[c, my_c, d, a, 1 - b], r2.at[c, d], t2s, fin.at[c], dev)

    def stage1(c):
        reduce0(c).wait_recv()
        for last in range(2):
            for d in range(2):
                a, b, _, _ = route(d)
                side = b if last else 1 - b
                ypart[c, my_c, d, 1 - a, side] = ypart[c, my_c, d, 1 - a, side] + r0[c, d, 1 - a, side]
        for last in range(2):
            for d in range(2):
                reduce1(c, d, last).start()
        for d in range(2):
            a, _, _, _ = route(d)
            ypart[c, my_c, d, a] = ypart[c, my_c, d, a] + r0[c, d, a]

    def stage2(c):
        wait_all(r1.at[c, 0], t1r.at[c])
        for d in range(2):
            a, b, _, _ = route(d)
            ypart[c, my_c, d, a, 1 - b] = ypart[c, my_c, d, a, 1 - b] + r1[c, d, 1 - b]
        for d in range(2):
            reduce2(c, d).start()

    def final(c):
        wait_all(r0.at[c, 0], fin.at[c])
        for d in range(2):
            a, b, _, _ = route(d)
            moe = ypart[c, my_c, d, a, b] + r1[c, d, b] + r2[c, d]
            x_own = own(c)[:, pl.ds(d * H, H)].astype(F32)
            shared = shy[:, pl.ds(c * T + d * H, H)].astype(F32)
            o_ref[:, pl.ds(c * T + d * H, H)] = (x_own + shared + moe).astype(BF16)

    for c in range(NCH):
        for h in range(NHB):
            s = A_STEPS + c * NHB + h
            w_wait(s)
            third = bdot(hid3[pl.ds(h * EG, EG)], ring[s % NS, 2].reshape(EG, 2 * T, T)).reshape(EB, 2 * CAP, T)
            for q in range(2):
                first = h * EB + q * EG
                out = bdot(hid[pl.ds(first, EG)], ring[s % NS, q].reshape(EG, 2 * T, T))
                out = (out + third[q * EG:(q + 1) * EG]).astype(BF16)
                for g in range(2):
                    for copy in range(2):
                        osc[g, copy, pl.ds(first, EG)] = out[:, g * CAP:(g + 1) * CAP]
            w_start(s + NS)
        if c >= 1:
            stage1(c - 1)
        for g in range(2):
            y = dot(comb[g], osc[g].reshape(2 * GROUP, T)) + dot(comb3[g], osc[g, 0].reshape(GROUP, T))
            y = y.reshape(2, 2, ROWS, T)
            for core in range(2):
                for x in range(2):
                    ypart[c, core, 0, x, g] = y[core, x, :, :H]
                    ypart[c, core, 1, g, x] = y[core, x, :, H:]
        reduce0(c).start()
        if c >= LAG2:
            stage2(c - LAG2)

    w_wait(SH_IN)
    for n in range(NF):
        acc = jnp.zeros((ROWS, T), F32)
        weights = ring[SH_IN % NS, n].reshape(NCH, T, T)
        for k in range(NCH):
            acc = acc + dot(own(k)[...], weights[k])
        hs[:, pl.ds(n * T, T)] = jax.nn.gelu(acc).astype(BF16)
    stage1(NCH - 1)
    stage2(NCH - 3)
    w_wait(SH_OUT)
    for c in range(NCH):
        acc = jnp.zeros((ROWS, T), F32)
        for j in range(NF):
            acc = acc + dot(hs[:, pl.ds(j * T, T)], ring[SH_OUT % NS, j, c // 2, c % 2])
        shy[:, pl.ds(c * T, T)] = acc.astype(BF16)
    stage2(NCH - 2)
    stage2(NCH - 1)
    for c in range(NCH):
        final(c)
    wait_all(mids.at[pl.ds(0, 7)], rts.at[0])
    wait_all(mgates.at[pl.ds(0, 7)], rts.at[1])
    wait_all(tok.at[pl.ds(0, 3), 0], g1s)
    wait_all(tok.at[pl.ds(0, 3), 0], g2s)
    wait_all(tok.at[pl.ds(0, 4)], gds)
    wait_all(r0, t0s)
    wait_all(r1, t1s)
    wait_all(r2, t2s)


def solution(mesh):
    def layer(tok_x, route_ids, route_gate, w_in, w_out, shared_in, shared_out):
        local = w_in.shape[0]
        any_space = pl.BlockSpec(memory_space=pl.ANY)
        dma = pltpu.SemaphoreType.DMA
        vmem = pltpu.VMEM
        return pl.pallas_call(
            kernel,
            out_shape=pltpu.VMEM((ROWS, WIDTH), BF16),
            in_specs=[any_space] * 8,
            out_specs=pl.BlockSpec(memory_space=pltpu.VMEM),
            scratch_shapes=[
                vmem((NCH, 2, 2, 2, ROWS, T), BF16),
                vmem((8, TOPK, ROWS), jnp.int32),
                vmem((8, TOPK, ROWS), F32),
                vmem((NS, NF, EG, 2, T, T), BF16),
                vmem((LOCAL, 2 * CAP, KS), BF16),
                vmem((LOCAL, 2 * CAP, FF), F32),
                vmem((LOCAL, 2 * CAP, 2 * T), BF16),
                vmem((LOCAL // 2, 4 * CAP, 2 * T), BF16),
                vmem((2, 2, LOCAL, CAP, T), BF16),
                vmem((2, LOCAL * CAP, GROUP), BF16),
                vmem((2, GROUP, 2 * GROUP), BF16),
                vmem((2, GROUP, GROUP), BF16),
                vmem((NCH, 2, 2, 2, 2, ROWS, H), F32),
                vmem((NCH, 2, 2, 2, ROWS, H), F32),
                vmem((NCH, 2, 2, ROWS, H), F32),
                vmem((NCH, 2, ROWS, H), F32),
                vmem((ROWS, FF), BF16),
                vmem((ROWS, WIDTH), BF16),
                dma((3,)), dma((2,)), dma((2,)),
                dma, dma((NK,)), dma, dma((NK,)), dma, dma((NK,)),
                dma((NS,)),
                dma, dma((NCH,)), dma, dma((NCH,)), dma, dma((NCH,)),
            ],
            compiler_params=pltpu.CompilerParams(
                collective_id=0, has_side_effects=True, vmem_limit_bytes=61_000_000),
            name='moe_layer',
        )(tok_x, route_ids.T, route_gate.T,
          w_in.reshape(local, WIDTH // T, T, FF), w_out.reshape(local, NF, T, WIDTH),
          w_out.reshape(local // 2, 2, NF, T, WIDTH),
          shared_in.reshape(EG, 2, T, FF), shared_out.reshape(NF, T, WIDTH))

    row_spec = P(('dp', 'ep'), None)
    expert_spec = P('ep', None, None)
    whole_spec = P(None, None)
    return jax.shard_map(layer, mesh=mesh,
                         in_specs=(row_spec, row_spec, row_spec, expert_spec, expert_spec, whole_spec, whole_spec),
                         out_specs=row_spec, check_vma=False)
```

profile of v0, /device:TPU:0, one launch (start us, length us, event | category | flops | bytes accessed | tf_op | source)
XLA Modules:
  0.0 47.9 jit_solution(7502888013787871086)
XLA Ops:
  0.0 47.2 %moe_layer.1 = bf16[64,2048]{1,0:T(8,128)(2,1)S(1)} custom-call(bf16[64,2048]{1,0:T(8,128)(2,1)} %x_ref.1, s32[8,64]{1,0:T(8,128)} %bitcast.9, f32[8,64]{1,0:T(8,128)} %bitcast.10, bf16[32,8,256,768]{3,2,1,0:T(8,128)(2,1)} %bitcast.2.win_ref, bf16[32,3,256,2048]{3,2,1,0:T(8,128)(2,1)} %bitcast.3.wout_ref, bf16[16,2,3,256,2048]{4,3,2,1,0:T(8,128)(2,1)} %bitcast.4.wpair_ref, ...), custom_call_target="tpu_custom_call" | custom-call | tf_op jit(solution)/shard_map/moe_layer/pallas_call | solution.py:366
  47.2 0.7 %copy.9 = bf16[64,2048]{1,0:T(8,128)(2,1)} copy(bf16[64,2048]{1,0:T(8,128)(2,1)S(1)} %moe_layer.1) | data formatting | bytes 524288
where the time goes:
time: 48.1 us; the launch traced here: 47.9 us
  Pallas kernels  47.2 us (98%)
  local copies, waits for them, and re-layouts  0.71 us (1%)
    pallas_call x1, Pallas kernels, layer(): pl.pallas_call(kernel, out_shape=pltpu.VMEM((ROWS, WIDTH), BF16), in_spec...  47.2 us

commit v1 on v0

--- a/solution.py
+++ b/solution.py
@@ -26,12 +26,10 @@
 NHB = LOCAL // EB
 NF = FF // T
 GROUP = 256
-NS = 13
+NS = 12
 A_STEPS = NK * NEG
-B_STEPS = NCH * NHB
-SH_IN = A_STEPS + B_STEPS
-SH_OUT = SH_IN + 1
-STEPS = SH_OUT + 1
+SLOT_IN = (A_STEPS + 4) % NS
+SLOT_OUT = SLOT_IN + 1
 LAG2 = 3
 
 
@@ -63,34 +61,29 @@
     def wait_all(ref, sem):
         pltpu.make_async_copy(ref, ref, sem).wait()
 
-    def w_copies(s):
-        slot = s % NS
-        if s == SH_OUT:
-            return [pltpu.make_async_copy(
-                sout_ref.at[:, :, pl.ds(c * T, T)], ring.at[slot, :, c // 2, c % 2], w_sem.at[slot]) for c in range(NCH)]
-        copies = []
-        for n in range(NF):
-            if s < A_STEPS:
-                k, eg = divmod(s, NEG)
-                src = win_ref.at[pl.ds(e_off + eg * EG, EG), pl.ds(2 * k, 2), :, pl.ds(n * T, T)]
-            elif s < SH_IN:
-                c, h = divmod(s - A_STEPS, NHB)
-                if n < 2:
-                    src = wout_ref.at[pl.ds(e_off + h * EB + n * EG, EG), pl.ds(0, 2), :, pl.ds(c * T, T)]
-                else:
-                    src = wpair_ref.at[pl.ds(e_off // 2 + h * EG, EG), :, 2, :, pl.ds(c * T, T)]
-            else:
-                src = sin_ref.at[:, :, :, pl.ds(n * T, T)]
-            copies.append(pltpu.make_async_copy(src, ring.at[slot, n], w_sem.at[slot]))
-        return copies
-
-    def w_start(s):
-        if s < STEPS:
-            for copy in w_copies(s):
-                copy.start()
-
-    def w_wait(s):
-        wait_all(ring.at[s % NS], w_sem.at[s % NS])
+    def start_all(slot, sources):
+        for n, src in enumerate(sources):
+            pltpu.make_async_copy(src, ring.at[slot, n], w_sem.at[slot]).start()
+
+    def start_a(slot, k, eg):
+        rows = pl.ds(e_off + eg * EG, EG)
+        start_all(slot, [win_ref.at[rows, pl.ds(2 * k, 2), :, pl.ds(n * T, T)] for n in range(NF)])
+
+    def start_b(slot, c, h):
+        cols = pl.ds(pl.multiple_of(c * T, T), T)
+        start_all(slot, [wout_ref.at[pl.ds(e_off + h * EB + n * EG, EG), pl.ds(0, 2), :, cols] for n in range(2)]
+                  + [wpair_ref.at[pl.ds(e_off // 2 + h * EG, EG), :, 2, :, cols]])
+
+    def start_in(slot):
+        start_all(slot, [sin_ref.at[:, :, :, pl.ds(n * T, T)] for n in range(NF)])
+
+    def start_out(slot):
+        for c in range(NCH):
+            pltpu.make_async_copy(
+                sout_ref.at[:, :, pl.ds(c * T, T)], ring.at[slot, :, c // 2, c % 2], w_sem.at[slot]).start()
+
+    def w_wait(slot):
+        wait_all(ring.at[slot], w_sem.at[slot])
 
     IDS, GATES = NCH, NCH + 1
 
@@ -145,11 +138,12 @@
     for i in items:
         load(i).start()
     hid3[...] = jnp.zeros_like(hid3)
+    hacc[...] = jnp.zeros_like(hacc)
     wait_all(tok.at[0], ld_sem.at[0])
     for i in routing:
         load(i).wait()
     for s in range(NS):
-        w_start(s)
+        start_a(s, s // NEG, s % NEG)
     pl.semaphore_wait(barrier, 7)
 
     def direct(i, r):
@@ -216,43 +210,73 @@
     send(3)
     send_on(1)
     share(0)
-    for k in range(NK):
+
+    def pick(k):
         wait_all(tok.at[2 * k], gdr.at[k])
         for h in range(2):
-            i = 2 * k + h
             for g in range(2):
-                rows = tok[i, :, :, g] if over_y(i) else tok[i, :, g]
+                rows = tok[2 * k + h, :, :, g] if h else tok[2 * k + h, :, g]
                 picked = dot(disp[g], rows.reshape(GROUP, T)).astype(BF16)
                 xs[:, pl.ds(g * CAP, CAP), pl.ds(h * T, T)] = picked.reshape(LOCAL, CAP, T)
-        for half in range(2):
-            steps = [k * NEG + half * 2 + q for q in range(2)]
-            for s in steps:
-                w_wait(s)
-            for s in steps:
-                eg = s % NEG
-                batch = pl.ds(eg * EG, EG)
-                for n in range(NF):
-                    cols = pl.ds(n * T, T)
-                    acc = bdot(xs[batch], ring[s % NS, n].reshape(EG, KS, T))
-                    if k > 0:
-                        acc = acc + hacc[batch, :, cols]
-                    if k < NK - 1:
-                        hacc[batch, :, cols] = acc
-                        continue
-                    act = jax.nn.gelu(acc).astype(BF16)
-                    if n < 2:
-                        hid[batch, :, cols] = act
-                    else:
-                        act = act.reshape(EG // 2, 2, 2 * CAP, T)
-                        for m in range(2):
-                            hid3[pl.ds(eg * EG // 2, EG // 2), pl.ds(m * 2 * CAP, 2 * CAP), pl.ds(m * T, T)] = act[:, m]
-            for s in steps:
-                w_start(s + NS)
-            if half == 0 and k < NK - 1:
-                if k == 0:
-                    send_on(2)
-                    send_on(3)
-                share(k + 1)
+
+    def first_product(t, slots, last):
+        for slot in slots:
+            w_wait(slot)
+        for q, slot in enumerate(slots):
+            eg = 2 * lax.rem(t, 2) + q if not last else 2 * (t % 2) + q
+            batch = pl.ds(eg * EG, EG)
+            for n in range(NF):
+                cols = pl.ds(n * T, T)
+                acc = bdot(xs[batch], ring[slot, n].reshape(EG, KS, T)) + hacc[batch, :, cols]
+                if not last:
+                    hacc[batch, :, cols] = acc
+                    continue
+                act = jax.nn.gelu(acc).astype(BF16)
+                if n < 2:
+                    hid[batch, :, cols] = act
+                else:
+                    act = act.reshape(EG // 2, 2, 2 * CAP, T)
+                    for m in range(2):
+                        hid3[pl.ds(eg * EG // 2, EG // 2), pl.ds(m * 2 * CAP, 2 * CAP), pl.ds(m * T, T)] = act[:, m]
+
+    def k_step(k, carry):
+        pick(k)
+
+        def half_step(half, carry):
+            t = 2 * k + half
+            first_product(t, [2 * t, 2 * t + 1], False)
+
+            @pl.when(t < 2)
+            def _():
+                for q in range(2):
+                    start_a(2 * t + q, NK - 1, 2 * t + q)
+
+            @pl.when(t >= 2)
+            def _():
+                for q in range(2):
+                    start_b(2 * t + q, t - 2, q)
+
+            @pl.when(t == 0)
+            def _():
+                send_on(2)
+                send_on(3)
+
+            for p in range(1, NK):
+                @pl.when(t == 2 * p - 2)
+                def _():
+                    share(p)
+
+            return carry
+
+        return lax.fori_loop(0, 2, half_step, carry)
+
+    lax.fori_loop(0, NK - 1, k_step, 0)
+    pick(NK - 1)
+    for t in (2 * NK - 2, 2 * NK - 1):
+        slots = [2 * t - NS, 2 * t + 1 - NS]
+        first_product(t, slots, True)
+        for q in range(2):
+            start_b(slots[q], t - 2, q)
 
     def route(d):
         if d == 0:
@@ -302,21 +326,35 @@
             shared = shy[:, pl.ds(c * T + d * H, H)].astype(F32)
             o_ref[:, pl.ds(c * T + d * H, H)] = (x_own + shared + moe).astype(BF16)
 
-    for c in range(NCH):
+    def chunk(c, carry):
+        base = lax.rem(2 * c + A_STEPS, NS)
         for h in range(NHB):
-            s = A_STEPS + c * NHB + h
-            w_wait(s)
-            third = bdot(hid3[pl.ds(h * EG, EG)], ring[s % NS, 2].reshape(EG, 2 * T, T)).reshape(EB, 2 * CAP, T)
+            slot = base + h
+            w_wait(slot)
+            third = bdot(hid3[pl.ds(h * EG, EG)], ring[slot, 2].reshape(EG, 2 * T, T)).reshape(EB, 2 * CAP, T)
             for q in range(2):
                 first = h * EB + q * EG
-                out = bdot(hid[pl.ds(first, EG)], ring[s % NS, q].reshape(EG, 2 * T, T))
+                out = bdot(hid[pl.ds(first, EG)], ring[slot, q].reshape(EG, 2 * T, T))
                 out = (out + third[q * EG:(q + 1) * EG]).astype(BF16)
                 for g in range(2):
                     for copy in range(2):
                         osc[g, copy, pl.ds(first, EG)] = out[:, g * CAP:(g + 1) * CAP]
-            w_start(s + NS)
-        if c >= 1:
+
+            @pl.when(c < 2)
+            def _():
+                start_b(slot, c + 6, h)
+
+            @pl.when(c == 2)
+            def _():
+                if h == 0:
+                    start_in(SLOT_IN)
+                else:
+                    start_out(SLOT_OUT)
+
+        @pl.when(c >= 1)
+        def _():
             stage1(c - 1)
+
         for g in range(2):
             y = dot(comb[g], osc[g].reshape(2 * GROUP, T)) + dot(comb3[g], osc[g, 0].reshape(GROUP, T))
             y = y.reshape(2, 2, ROWS, T)
@@ -325,23 +363,29 @@
                     ypart[c, core, 0, x, g] = y[core, x, :, :H]
                     ypart[c, core, 1, g, x] = y[core, x, :, H:]
         reduce0(c).start()
-        if c >= LAG2:
+
+        @pl.when(c >= LAG2)
+        def _():
             stage2(c - LAG2)
 
-    w_wait(SH_IN)
+        return carry
+
+    lax.fori_loop(0, NCH, chunk, 0)
+
+    w_wait(SLOT_IN)
     for n in range(NF):
         acc = jnp.zeros((ROWS, T), F32)
-        weights = ring[SH_IN % NS, n].reshape(NCH, T, T)
+        weights = ring[SLOT_IN, n].reshape(NCH, T, T)
         for k in range(NCH):
             acc = acc + dot(own(k)[...], weights[k])
         hs[:, pl.ds(n * T, T)] = jax.nn.gelu(acc).astype(BF16)
     stage1(NCH - 1)
     stage2(NCH - 3)
-    w_wait(SH_OUT)
+    w_wait(SLOT_OUT)
     for c in range(NCH):
         acc = jnp.zeros((ROWS, T), F32)
         for j in range(NF):
-            acc = acc + dot(hs[:, pl.ds(j * T, T)], ring[SH_OUT % NS, j, c // 2, c % 2])
+            acc = acc + dot(hs[:, pl.ds(j * T, T)], ring[SLOT_OUT, j, c // 2, c % 2])
         shy[:, pl.ds(c * T, T)] = acc.astype(BF16)
     stage2(NCH - 2)
     stage2(NCH - 1)
@@ -393,7 +437,7 @@
                 dma, dma((NCH,)), dma, dma((NCH,)), dma, dma((NCH,)),
             ],
             compiler_params=pltpu.CompilerParams(
-                collective_id=0, has_side_effects=True, vmem_limit_bytes=61_000_000),
+                collective_id=0, has_side_effects=True, vmem_limit_bytes=58_000_000),
             name='moe_layer',
         )(tok_x, route_ids.T, route_gate.T,
           w_in.reshape(local, WIDTH // T, T, FF), w_out.reshape(local, NF, T, WIDTH),

time: 48.1 us -> 48.6 us (1.010)
  Pallas kernels: 47.2 us -> 47.7 us
where the time goes in v1:
time: 48.6 us; the launch traced here: 48.4 us
  Pallas kernels  47.7 us (98%)
  local copies, waits for them, and re-layouts  0.71 us (1%)
    pallas_call x1, Pallas kernels, layer(): pl.pallas_call(kernel, out_shape=pltpu.VMEM((ROWS, WIDTH), BF16), in_spec...  47.7 us

profile of v1, /device:TPU:0, one launch (start us, length us, event | category | flops | bytes accessed | tf_op | source)
XLA Modules:
  0.0 48.4 jit_solution(3094964934815876120)
XLA Ops:
  0.0 47.7 %moe_layer.1 = bf16[64,2048]{1,0:T(8,128)(2,1)S(1)} custom-call(bf16[64,2048]{1,0:T(8,128)(2,1)} %x_ref.1, s32[8,64]{1,0:T(8,128)} %bitcast.9, f32[8,64]{1,0:T(8,128)} %bitcast.10, bf16[32,8,256,768]{3,2,1,0:T(8,128)(2,1)} %bitcast.2.win_ref, bf16[32,3,256,2048]{3,2,1,0:T(8,128)(2,1)} %bitcast.3.wout_ref, bf16[16,2,3,256,2048]{4,3,2,1,0:T(8,128)(2,1)} %bitcast.4.wpair_ref, ...), custom_call_target="tpu_custom_call" | custom-call | tf_op jit(solution)/shard_map/moe_layer/pallas_call | solution.py:410
  47.7 0.7 %copy.9 = bf16[64,2048]{1,0:T(8,128)(2,1)} copy(bf16[64,2048]{1,0:T(8,128)(2,1)S(1)} %moe_layer.1) | data formatting | bytes 524288

commit v2 on v0

--- a/solution.py
+++ b/solution.py
@@ -148,8 +148,6 @@
     wait_all(tok.at[0], ld_sem.at[0])
     for i in routing:
         load(i).wait()
-    for s in range(NS):
-        w_start(s)
     pl.semaphore_wait(barrier, 7)
 
     def direct(i, r):
@@ -175,6 +173,8 @@
     for r in (3, 2, 1):
         for i in (0, 1):
             direct(i, r).start()
+    for s in range(NS):
+        w_start(s)
     send(1)
     wait_all(mids.at[pl.ds(0, 7)], rtr.at[0])
     wait_all(mgates.at[pl.ds(0, 7)], rtr.at[1])
@@ -317,6 +317,8 @@
             w_start(s + NS)
         if c >= 1:
             stage1(c - 1)
+        if c >= LAG2:
+            stage2(c - LAG2)
         for g in range(2):
             y = dot(comb[g], osc[g].reshape(2 * GROUP, T)) + dot(comb3[g], osc[g, 0].reshape(GROUP, T))
             y = y.reshape(2, 2, ROWS, T)
@@ -325,8 +327,6 @@
                     ypart[c, core, 0, x, g] = y[core, x, :, :H]
                     ypart[c, core, 1, g, x] = y[core, x, :, H:]
         reduce0(c).start()
-        if c >= LAG2:
-            stage2(c - LAG2)
 
     w_wait(SH_IN)
     for n in range(NF):

time: 48.1 us -> 47.9 us (level)
  no operation moved by 1% of the time
where the time goes in v2:
time: 47.9 us; the launch traced here: 47.7 us
  Pallas kernels  47 us (98%)
  local copies, waits for them, and re-layouts  0.71 us (1%)
    pallas_call x1, Pallas kernels, layer(): pl.pallas_call(kernel, out_shape=pltpu.VMEM((ROWS, WIDTH), BF16), in_spec...  47 us

profile of v2, /device:TPU:0, one launch (start us, length us, event | category | flops | bytes accessed | tf_op | source)
XLA Modules:
  0.0 47.7 jit_solution(6174006964109832302)
XLA Ops:
  0.0 47.0 %moe_layer.1 = bf16[64,2048]{1,0:T(8,128)(2,1)S(1)} custom-call(bf16[64,2048]{1,0:T(8,128)(2,1)} %x_ref.1, s32[8,64]{1,0:T(8,128)} %bitcast.9, f32[8,64]{1,0:T(8,128)} %bitcast.10, bf16[32,8,256,768]{3,2,1,0:T(8,128)(2,1)} %bitcast.2.win_ref, bf16[32,3,256,2048]{3,2,1,0:T(8,128)(2,1)} %bitcast.3.wout_ref, bf16[16,2,3,256,2048]{4,3,2,1,0:T(8,128)(2,1)} %bitcast.4.wpair_ref, ...), custom_call_target="tpu_custom_call" | custom-call | tf_op jit(solution)/shard_map/moe_layer/pallas_call | solution.py:366
  47.0 0.7 %copy.9 = bf16[64,2048]{1,0:T(8,128)(2,1)} copy(bf16[64,2048]{1,0:T(8,128)(2,1)S(1)} %moe_layer.1) | data formatting | bytes 524288

commit v3 on v2

--- a/solution.py
+++ b/solution.py
@@ -151,7 +151,7 @@
     pl.semaphore_wait(barrier, 7)
 
     def direct(i, r):
-        return remote(own(i), own(i), g1s, g2r.at[0], peer(r))
+        return remote(own(i), own(i), g1s, g2r.at[i // 2], peer(r))
 
     def send(p):
         for i in (2 * p, 2 * p + 1):
@@ -163,19 +163,19 @@
             gather2(i).start()
 
     def share(p):
-        wait_all(tok.at[pl.ds(0, 3), 0, 0] if p == 0 else tok.at[2 * p, 0], g2r.at[p])
+        wait_all(tok.at[pl.ds(0, 3), 0, 0] if p < 2 else tok.at[2 * p, 0], g2r.at[p])
         for i in (2 * p, 2 * p + 1):
             gatherd(i).start()
 
     for r in (3, 7, 1, 2, 5, 6, 4):
         for i in routing:
             tell(i, r).start()
-    for r in (3, 2, 1):
-        for i in (0, 1):
-            direct(i, r).start()
+    for p in range(2):
+        for r in (3, 2, 1):
+            for i in (2 * p, 2 * p + 1):
+                direct(i, r).start()
     for s in range(NS):
         w_start(s)
-    send(1)
     wait_all(mids.at[pl.ds(0, 7)], rtr.at[0])
     wait_all(mgates.at[pl.ds(0, 7)], rtr.at[1])
 
@@ -214,7 +214,6 @@
 
     send(2)
     send(3)
-    send_on(1)
     share(0)
     for k in range(NK):
         wait_all(tok.at[2 * k], gdr.at[k])
@@ -249,10 +248,10 @@
             for s in steps:
                 w_start(s + NS)
             if half == 0 and k < NK - 1:
+                share(k + 1)
                 if k == 0:
                     send_on(2)
                     send_on(3)
-                share(k + 1)
 
     def route(d):
         if d == 0:
@@ -349,8 +348,8 @@
         final(c)
     wait_all(mids.at[pl.ds(0, 7)], rts.at[0])
     wait_all(mgates.at[pl.ds(0, 7)], rts.at[1])
-    wait_all(tok.at[pl.ds(0, 3), 0], g1s)
-    wait_all(tok.at[pl.ds(0, 3), 0], g2s)
+    wait_all(tok.at[pl.ds(0, 2)], g1s)
+    wait_all(tok.at[0], g2s)
     wait_all(tok.at[pl.ds(0, 4)], gds)
     wait_all(r0, t0s)
     wait_all(r1, t1s)

time: 47.9 us -> 48.3 us (level)
  Pallas kernels: 47 us -> 47.5 us
where the time goes in v3:
time: 48.3 us; the launch traced here: 48.2 us
  Pallas kernels  47.5 us (98%)
  local copies, waits for them, and re-layouts  0.71 us (1%)
    pallas_call x1, Pallas kernels, layer(): pl.pallas_call(kernel, out_shape=pltpu.VMEM((ROWS, WIDTH), BF16), in_spec...  47.5 us

profile of v3, /device:TPU:0, one launch (start us, length us, event | category | flops | bytes accessed | tf_op | source)
XLA Modules:
  0.0 48.2 jit_solution(4123658343939266921)
XLA Ops:
  0.0 47.5 %moe_layer.1 = bf16[64,2048]{1,0:T(8,128)(2,1)S(1)} custom-call(bf16[64,2048]{1,0:T(8,128)(2,1)} %x_ref.1, s32[8,64]{1,0:T(8,128)} %bitcast.9, f32[8,64]{1,0:T(8,128)} %bitcast.10, bf16[32,8,256,768]{3,2,1,0:T(8,128)(2,1)} %bitcast.2.win_ref, bf16[32,3,256,2048]{3,2,1,0:T(8,128)(2,1)} %bitcast.3.wout_ref, bf16[16,2,3,256,2048]{4,3,2,1,0:T(8,128)(2,1)} %bitcast.4.wpair_ref, ...), custom_call_target="tpu_custom_call" | custom-call | tf_op jit(solution)/shard_map/moe_layer/pallas_call | solution.py:365
  47.5 0.7 %copy.9 = bf16[64,2048]{1,0:T(8,128)(2,1)} copy(bf16[64,2048]{1,0:T(8,128)(2,1)S(1)} %moe_layer.1) | data formatting | bytes 524288
